TPU v7x, 256 devices: a whole 4x4x8 slice. The times are simulated.
256 devices in a mesh: batch: 32 (over z_hi, y, core), gene: 8 (over x, z_lo).
Axes of the slice: x: 4, y: 4, z: 8 (z_hi: 4, z_lo: 2; z = z_hi * 2 + z_lo), core: 2. Of those that a mesh axis runs over, the one named last changes fastest.
Arguments:
- umi_counts: int32 [32768, 8192], P('batch', 'gene'), may hold values from 0 to 65535
- cell_donors: int32 [32768], P('batch'), may hold values from 0 to 127
- cell_types: int32 [32768], P('batch'), may hold values from 0 to 23
- live_cells: int32 [32], P('batch'), may hold values from 1 to 1024, 20480 in all
- dosages: int32 [128, 4096], P(None, 'batch'), may hold values from 0 to 2
Outputs:
- scores: bfloat16 [24, 8192, 4096], P(None, ('gene', 'batch'))
All inputs are finite; a program needn't handle non-finite values. No bound on the sum of `live_cells` on one device may be relied on, other than what follows from the above.
Results may differ from a plain program's by a relative error of at most 0.0069.
Values may be sent and summed in bfloat16 or wider, within the bound.
A program may use at most 128 MiB of HBM per device.

v0:
```python
import jax
import jax.numpy as jnp
from jax import lax
from jax.sharding import Mesh
from jax.sharding import PartitionSpec as P

TYPES = 24
DONORS = 128
BATCH = ("batch_0", "batch_1", "batch_2")
BATCH_GENE = ("batch_0", "batch_1", "batch_2", "gene_0", "gene_1")
GENE = ("gene_0", "gene_1")
GENE_BATCH = ("gene_0", "gene_1", "batch_0", "batch_1", "batch_2")


def in_blocks(value, dim, count):
    dims = value.shape
    tiles = value.reshape(*dims[:dim], count, dims[dim] // count, *dims[dim + 1 :])
    return jnp.moveaxis(tiles, dim, 0)


def summed_rows_2(value, chips, core, dim):
    sizes = (lax.axis_size(chips), lax.axis_size(core))
    tiles = in_blocks(value, dim, sizes[0] * sizes[1])
    inside = tiles.shape[1:]
    tiles = tiles.reshape(*sizes, *inside).swapaxes(0, 1).reshape(-1, *inside)
    tiles = lax.psum_scatter(tiles, core, scatter_dimension=0, tiled=True)
    return lax.psum_scatter(tiles, chips, scatter_dimension=0, tiled=True)[0]


def one_axis_at_a_time(value, axes):
    for axis in axes:
        value = lax.psum(value, axis)
    return value


def one_hot_rows(group_ids, total_groups):
    columns = jnp.arange(total_groups, dtype=jnp.int32)
    return (group_ids[:, None] == columns[None, :]).astype(jnp.bfloat16)


def standardize_dosage(block_dosage):
    genotype = block_dosage.astype(jnp.float32)
    centred = genotype - jnp.mean(genotype, axis=0, keepdims=True)
    return (centred * lax.rsqrt(jnp.mean(centred * centred, axis=0, keepdims=True) + 1e-06)).astype(
        jnp.bfloat16
    )


def on_device(umi_counts, cell_donors, cell_types, live_cells, dosages):
    total_groups = TYPES * DONORS
    cell_slots = umi_counts.shape[0]
    genes_block = umi_counts.shape[1]
    batch_count = lax.axis_size(BATCH)
    genes_local = genes_block // batch_count
    slot_index = jnp.arange(cell_slots, dtype=jnp.int32)
    alive_mask = slot_index < live_cells[0]
    cell_group = jnp.where(alive_mask, cell_types * DONORS + cell_donors, -1)
    rounded = umi_counts.astype(jnp.bfloat16)
    table = one_hot_rows(cell_group, total_groups)
    pseudo = summed_rows_2(
        lax.dot_general(
            rounded, table, (((0,), (0,)), ((), ())), preferred_element_type=jnp.float32
        ),
        ("batch_0", "batch_1"),
        "batch_2",
        0,
    )
    partial_library = jnp.sum(pseudo, axis=0)
    library = jnp.maximum(one_axis_at_a_time(partial_library, BATCH_GENE), 1.0)
    logged = jnp.log1p(10000.0 * pseudo / library[None, :]).reshape(genes_local, TYPES, DONORS)
    centred = logged - jnp.mean(logged, axis=2, keepdims=True)
    standard = (
        centred * lax.rsqrt(jnp.mean(centred * centred, axis=2, keepdims=True) + 1e-06)
    ).astype(jnp.bfloat16)
    standard_rows = jnp.transpose(standard, (1, 0, 2)).reshape(TYPES * genes_local, DONORS)
    factor = DONORS ** (-0.5)
    geno_local = standardize_dosage(dosages)
    geno_piece = lax.all_gather(geno_local, BATCH, axis=1, tiled=True)
    product = jnp.dot(standard_rows, geno_piece, preferred_element_type=jnp.float32) * factor
    return product.reshape(TYPES, genes_local, geno_piece.shape[1]).astype(jnp.bfloat16)


def solution(mesh):
    torus = Mesh(
        mesh.devices.reshape(4, 4, 2, 4, 2), ("batch_0", "batch_1", "batch_2", "gene_0", "gene_1")
    )
    return jax.shard_map(
        on_device,
        mesh=torus,
        in_specs=(P(BATCH, GENE), P(BATCH), P(BATCH), P(BATCH), P(None, BATCH)),
        out_specs=P(None, GENE_BATCH, None),
        check_vma=False,
    )
```

profile of v0, /device:TPU:1, one launch (start us, length us, event | category | flops | bytes accessed | tf_op | source)
XLA Modules:
  0.0 251.8 jit_solution(15902992954588551847)
XLA Ops:
  7.4 0.0 reduce-scatter.3.cloned.1.call-start
  8.0 0.7 add_select_fusion
  8.7 12.0 %fusion = f32[3072,1024]{0,1:T(8,128)} fusion(s32[1024]{0:T(1024)S(1)} %add_select_fusion, s32[1024,1024]{1,0:T(8,128)} %param.5), kind=kOutput, calls=%fused_computation.2 | convolution fusion | flops 6446645248 | bytes 16781312 | tf_op jit(solution)/shard_map/dot_general | solution.py:61
  20.7 10.8 %copy.6 = f32[16,2,32,3072]{3,2,0,1:T(8,128)} copy(f32[16,2,32,3072]{3,2,1,0:T(8,128)} %bitcast.21) | data formatting | bytes 25165824 | tf_op jit(solution)/shard_map/reshape;reshape | solution.py:25
  31.5 0.0 reduce-scatter.3.cloned.1.call-update
  31.5 0.0 copy-start
  31.6 0.0 reduce-scatter.5.cloned.1.call-start
  31.6 30.5 %reduce-scatter.3.cloned.1.call-done = f32[16,32,3072]{2,1,0:T(8,128)} async-done(((f32[32,32,3072]{2,1,0:T(8,128)}), f32[16,32,3072]{2,1,0:T(8,128)}) %reduce-scatter.3.cloned.1.call-update) | async-done | bytes 6291472 | tf_op jit(solution)/shard_map/reduce_scatter | solution.py:26
  62.1 0.0 reduce-scatter.5.cloned.1.call-update
  62.1 0.0 all-gather.2.cloned.1.call-start
  62.2 0.0 copy-done
  62.3 0.6 multiply_convert_fusion.2
  62.9 0.0 all-gather.2.cloned.1.call-update
  62.9 116.2 %reduce-scatter.5.cloned.1.call-done = f32[1,32,3072]{2,1,0:T(8,128)} async-done(((f32[16,32,3072]{2,1,0:T(8,128)}), f32[1,32,3072]{2,1,0:T(8,128)}) %reduce-scatter.5.cloned.1.call-update) | async-done | bytes 393232 | tf_op jit(solution)/shard_map/reduce_scatter | solution.py:27
  179.2 1.0 multiply_bitcast_fusion
  180.2 0.1 copy.8
  180.3 14.0 %psum.35 = f32[3072]{0:T(1024)S(1)} all-reduce(f32[3072]{0:T(1024)S(1)} %get-tuple-element.6), channel_id=1, replica_groups=mesh['batch_0'=4,'batch_1'=4,'batch_2'=2,'gene_0'=4,'gene_1'=2] {'batch_0'}, use_global_device_ids=true, to_apply=%region_3.4 | all-reduce | flops 3072 | bytes 24576 | tf_op jit(solution)/shard_map/psum | solution.py:32
  194.3 14.0 %psum.36 = f32[3072]{0:T(1024)S(1)} all-reduce(f32[3072]{0:T(1024)S(1)} %psum.35), channel_id=1, replica_groups=mesh['batch_0'=4,'batch_1'=4,'batch_2'=2,'gene_0'=4,'gene_1'=2] {'batch_1'}, use_global_device_ids=true, to_apply=%region_4.5 | all-reduce | flops 3072 | bytes 24576 | tf_op jit(solution)/shard_map/psum | solution.py:32
  208.3 11.5 %psum.37 = f32[3072]{0:T(1024)S(1)} all-reduce(f32[3072]{0:T(1024)S(1)} %psum.36), channel_id=1, replica_groups=mesh['batch_0'=4,'batch_1'=4,'batch_2'=2,'gene_0'=4,'gene_1'=2] {'batch_2'}, use_global_device_ids=true, to_apply=%region_5.6 | all-reduce | flops 3072 | bytes 24576 | tf_op jit(solution)/shard_map/psum | solution.py:32
  219.8 13.0 %psum.38 = f32[3072]{0:T(1024)S(1)} all-reduce(f32[3072]{0:T(1024)S(1)} %psum.37), channel_id=1, replica_groups=mesh['batch_0'=4,'batch_1'=4,'batch_2'=2,'gene_0'=4,'gene_1'=2] {'gene_0'}, use_global_device_ids=true, to_apply=%region_6.7 | all-reduce | flops 3072 | bytes 24576 | tf_op jit(solution)/shard_map/psum | solution.py:32
  232.8 5.0 %psum.39 = f32[3072]{0:T(1024)S(1)} all-reduce(f32[3072]{0:T(1024)S(1)} %psum.38), channel_id=1, replica_groups=mesh['batch_0'=4,'batch_1'=4,'batch_2'=2,'gene_0'=4,'gene_1'=2] {'gene_1'}, use_global_device_ids=true, to_apply=%region_7.8 | all-reduce | flops 3072 | bytes 24576 | tf_op jit(solution)/shard_map/psum | solution.py:32
  237.7 0.2 fusion.4
  238.0 0.3 multiply_reduce_fusion
  238.3 0.3 multiply_convert_fusion.1
  238.6 0.0 all-gather.2.cloned.1.call-done
  238.6 5.7 %multiply_convert_fusion = bf16[768,4096]{1,0:T(8,128)(2,1)} fusion(bf16[768,128]{1,0:T(8,128)(2,1)S(1)} %bitcast.25, bf16[128,4096]{1,0:T(8,128)(2,1)} %all-gather.2.cloned.1.call-done), kind=kOutput, calls=%fused_computation | convolution fusion | flops 811597824 | bytes 7536640 | tf_op jit(solution)/shard_map/dot_general | solution.py:79
  (7 shorter events, 0.1 us)
Async XLA Ops:
  7.4 54.7 %reduce-scatter.3.cloned.1.call-start = ((), (), s32[]{:S(2)}) async-start(), calls=%async_computation.2 | async-start | bytes 18874368 | tf_op jit(solution)/shard_map/reduce_scatter | solution.py:26
  31.5 30.6 %copy-start = (s32[128,128]{1,0:T(8,128)S(1)}, s32[128,128]{1,0:T(8,128)}, u32[]{:S(2)}) copy-start(s32[128,128]{1,0:T(8,128)} %param.9) | copy-start | bytes 196612
  31.6 147.6 %reduce-scatter.5.cloned.1.call-start = ((), (), s32[]{:S(2)}) async-start(), calls=%async_computation.3 | async-start | bytes 6684672 | tf_op jit(solution)/shard_map/reduce_scatter | solution.py:27
  62.1 176.5 %all-gather.2.cloned.1.call-start = ((), (), s32[]{:S(2)}) async-start(), calls=%async_computation.4 | async-start | bytes 1081344 | tf_op jit(solution)/shard_map/all_gather | solution.py:78
Sparse Core Ops, SparseCore 0:
  31.7 30.3 reduce-scatter.2
  65.8 113.2 reduce-scatter.4
Sparse Core Ops, SparseCore 1:
  65.1 63.2 all-gather.1
where the time goes:
time: 256 us; the launch traced here: 252 us
  waiting for transfers between devices  147 us (57%)
  blocking collectives  57.4 us (22%)
  matrix products  17.7 us (7%)
  between operations  15.6 us (6%)
  local copies, waits for them, and re-layouts  10.9 us (4%)
  other arithmetic  3.33 us (1%)
    reduce_scatter x1, waiting for transfers between devices, summed_rows_2(): return lax.psum_scatter(tiles, chips, scatter_dimension=0, tiled=True)[0]  116 us
    psum x5, blocking collectives, one_axis_at_a_time(): value = lax.psum(value, axis)  57.4 us
    reduce_scatter x1, waiting for transfers between devices, summed_rows_2(): tiles = lax.psum_scatter(tiles, core, scatter_dimension=0, tiled=True)  30.5 us
    dot_general x1, matrix products, on_device(): lax.dot_general(rounded, table, (((0,), (0,)), ((), ())), preferred_eleme...  12 us
    another operation x1, local copies, waits for them, and re-layouts, summed_rows_2(): tiles = tiles.reshape(*sizes, *inside).swapaxes(0, 1).reshape(-1, *inside)  10.8 us
    dot_general x1, matrix products, on_device(): jnp.dot(standard_rows, geno_piece, preferred_element_type=jnp.float32)  5.72 us
  transfers between devices with their start and end apart: 3, of which 2 were waited for; matrix products, arithmetic and copies ran while one was open for 1% of the time, Pallas kernels for 0%

commit v1 on v0

v1 whole, which is shorter than its diff:
```python
import jax
import jax.numpy as jnp
from jax import lax
from jax.experimental import pallas as pl
from jax.experimental.pallas import tpu as pltpu
from jax.sharding import Mesh
from jax.sharding import PartitionSpec as P

TYPES = 24
DONORS = 128
AXES = ("batch_0", "batch_1", "batch_2", "gene_0", "gene_1")
SIZES = {"batch_0": 4, "batch_1": 4, "batch_2": 2, "gene_0": 4, "gene_1": 2}
Z, Y, CORE, X, ZLO = AXES
BATCH = AXES[:3]
GENE = AXES[3:]
MESH = pl.DeviceIdType.MESH
F32 = jnp.float32
BF16 = jnp.bfloat16

CHUNKS = (2, 1, 3, 0)
SLOTS = tuple((dy, dc) for dy in (0, 1, 3, 2) for dc in (0, 1))
ZSLOTS = tuple((oz, ol) for oz in range(4) for ol in range(2))
OFFS = (1, 2, 3)
STRIP = 32
NT = (((1,), (1,)), ((), ()))
TN = (((0,), (0,)), ((), ()))


def three_parts(value):
    first = value.astype(BF16)
    rest = value - first.astype(F32)
    second = rest.astype(BF16)
    third = (rest - second.astype(F32)).astype(BF16)
    return first, second, third


def gather_kernel(
    live_ref, umi_ref, donors_ref, types_ref, dosages_ref,
    std_ref, geno_ref,
    xin, sendb, recvb, codeb, onehot, mask, wide, acc, zsend, zrecv, rows, gown, gbuf, lsend, lrx, lrz, lry,
    in_sem, d_send, d_recv, c_send, c_recv, g_send, g_recv, l_send, l_recv, z_send, z_recv, out_sem,
):
    at = {axis: lax.axis_index(axis) for axis in AXES}
    zi, yi, ci, xi = at[Z], at[Y], at[CORE], at[X]

    def moved(axis, offset):
        return lax.rem(at[axis] + offset, SIZES[axis])

    def peer(**offsets):
        return {axis: moved(axis, offset) for axis, offset in offsets.items() if offset}

    def remote(src, dst, send, recv, device):
        return pltpu.make_async_remote_copy(
            src_ref=src, dst_ref=dst, send_sem=send, recv_sem=recv, device_id=device, device_id_type=MESH
        )

    y_peers = [peer(batch_1=dy, batch_2=dc) for dy, dc in SLOTS]
    z_peers = [peer(batch_0=oz, gene_1=ol) for oz, ol in ZSLOTS]
    x_peers = [peer(gene_0=o) for o in OFFS]

    loads = []
    for c, off in enumerate(CHUNKS):
        col = pl.multiple_of(moved(Z, off) * 256, 256)
        load = pltpu.make_async_copy(umi_ref.at[:, pl.ds(col, 256)], xin.at[c], in_sem.at[c])
        load.start()
        loads.append(load)

    barrier = pltpu.get_barrier_semaphore()
    for device in y_peers[1:] + z_peers[1:] + x_peers:
        pl.semaphore_signal(barrier, inc=1, device_id=device, device_id_type=MESH)

    slot = lax.broadcasted_iota(jnp.int32, (8, 128), 0) * 128 + lax.broadcasted_iota(jnp.int32, (8, 128), 1)
    alive = slot < live_ref[0]
    types = types_ref[...]
    donors = donors_ref[...]
    codeb[0] = jnp.where(alive, ((types >> 3) * DONORS + donors) * 8 + (types & 7), -8)

    genotype = dosages_ref[...].astype(F32)
    centred = genotype - jnp.mean(genotype, axis=0, keepdims=True)
    gown[...] = (centred * lax.rsqrt(jnp.mean(centred * centred, axis=0, keepdims=True) + 1e-06)).astype(BF16)
    quarter = pl.ds(pl.multiple_of(xi * 32, 32), 32)
    gbuf[zi, yi, ci, quarter, :] = gown[quarter, :]
    rows[...] = jnp.zeros_like(rows)
    lane = lax.broadcasted_iota(jnp.int32, (STRIP, 128), 1)
    low = lane < 64
    even = (lane & 32) == 0

    def pack(c):
        def body(i, _):
            r0 = pl.multiple_of(i * STRIP, STRIP)
            total = None
            for h in range(2):
                x = [
                    xin[c, pl.ds(pl.multiple_of(k * 256 + r0, STRIP), STRIP), pl.ds(h * 128, 128)].astype(F32)
                    for k in range(4)
                ]
                a = [None] * 4
                for k in range(2):
                    a[k] = jnp.where(low, x[k], pltpu.roll(x[k + 2], 64, 1))
                    a[k + 2] = jnp.where(low, pltpu.roll(x[k], 64, 1), x[k + 2])
                for k in (0, 2):
                    for q, piece in (
                        (k, jnp.where(even, a[k], pltpu.roll(a[k + 1], 32, 1))),
                        (k + 1, jnp.where(even, pltpu.roll(a[k], 96, 1), a[k + 1])),
                    ):
                        rounded = piece.astype(BF16)
                        sendb[c, h * 4 + q, pl.ds(r0, STRIP), :] = rounded
                        exact = rounded.astype(F32)
                        total = exact if total is None else total + exact
            rows[pl.ds(r0, STRIP), :] += total
            return 0

        lax.fori_loop(0, 256 // STRIP, body, 0)

    own = yi * 2 + ci
    pending = []

    def start(copy):
        copy.start()
        pending.append(copy)
        return copy

    def send_pieces(c):
        for k in (2, 3, 4, 5, 6, 7, 1):
            dy, dc = SLOTS[k]
            piece = moved(Y, dy) * 2 + moved(CORE, dc)
            start(remote(sendb.at[c, piece], recvb.at[c, k], d_send.at[c, k], d_recv.at[c, k], y_peers[k]))

    loads[0].wait()
    pack(0)
    pl.semaphore_wait(barrier, 7 + 7 + 3)
    send_pieces(0)
    code_copies = [
        start(remote(codeb.at[0], codeb.at[k], c_send.at[k], c_recv.at[k], y_peers[k])) for k in range(1, 8)
    ]
    g1 = [
        start(remote(gbuf.at[zi, yi, ci, quarter], gbuf.at[zi, yi, ci, quarter], g_send.at[0, o], g_recv.at[0, o], {Z: moved(Z, off)}))
        for o, off in enumerate(OFFS)
    ]
    loads[1].wait()
    pack(1)
    send_pieces(1)
    for c in (2, 3):
        loads[c].wait()
        pack(c)
    for c in range(4):
        recvb[c, 0] = sendb[c, own]

    select = jnp.where(
        lax.broadcasted_iota(jnp.int32, (8, 128), 1) // 32 == lax.broadcasted_iota(jnp.int32, (8, 128), 0), 1.0, 0.0
    ).astype(BF16)
    sums = sum(lax.dot_general(select, part, NT, preferred_element_type=F32) for part in three_parts(rows[...]))
    part_library = None
    for k in range(4):
        type_row = jnp.concatenate([jnp.where(alive, types, -1)[2 * k + i : 2 * k + i + 1, :] for i in range(2)], axis=1)
        donor_row = jnp.concatenate([donors[2 * k + i : 2 * k + i + 1, :] for i in range(2)], axis=1)
        own_type = lax.broadcasted_iota(jnp.int32, (32, 256), 0) == type_row
        own_donor = jnp.where(lax.broadcasted_iota(jnp.int32, (DONORS, 256), 0) == donor_row, 1.0, 0.0).astype(BF16)
        for part in three_parts(sums[k : k + 1, :]):
            left = jnp.where(own_type, part.astype(F32), 0.0).astype(BF16)
            term = lax.dot_general(left, own_donor, NT, preferred_element_type=F32)
            part_library = term if part_library is None else part_library + term
    lsend[0] = part_library
    lx = [start(remote(lsend.at[0], lrx.at[o], l_send.at[0, o], l_recv.at[0, o], x_peers[o])) for o in range(3)]

    block = lax.broadcasted_iota(jnp.int32, (128, 128), 1) // 32

    def build(s):
        code = codeb[s]
        columns = jnp.transpose((code & 7).astype(F32)).astype(jnp.int32)
        group = code >> 3
        for g in range(8):
            match = lax.broadcasted_iota(jnp.int32, (384, 128), 0) == group[g : g + 1, :]
            onehot[s, :, pl.ds(g * 128, 128)] = jnp.where(match, 1.0, 0.0).astype(BF16)
            column = columns[:, g : g + 1]
            for h in range(2):
                mask[s, pl.ds(g * 128, 128), pl.ds(h * 128, 128)] = jnp.where(column == block + 4 * h, 1.0, 0.0).astype(BF16)

    build(0)
    for copy in g1:
        copy.wait_recv()
    g2 = [
        start(remote(gbuf.at[:, yi, ci, quarter], gbuf.at[:, yi, ci, quarter], g_send.at[1, o], g_recv.at[1, o], {Y: moved(Y, off)}))
        for o, off in enumerate(OFFS)
    ]
    for copy in code_copies:
        copy.wait_recv()
    lax.fori_loop(1, 8, lambda s, _: (build(s), 0)[1], 0)
    send_pieces(2)
    for copy in lx:
        copy.wait_recv()
    lsend[1] = lsend[0] + lrx[0] + lrx[1] + lrx[2]
    lz = [start(remote(lsend.at[1], lrz.at[k], l_send.at[1, k], l_recv.at[1, k], z_peers[k])) for k in range(1, 8)]

    quad = lax.broadcasted_iota(jnp.int32, (STRIP, 128), 1) // 32

    def group_sums(c):
        acc[...] = jnp.zeros_like(acc)

        def body(s, _):
            @pl.when(s > 0)
            def _():
                remote(recvb.at[c, s], recvb.at[c, s], d_send.at[c, s], d_recv.at[c, s], y_peers[1]).wait_recv()

            def widen(i, _):
                r0 = pl.multiple_of(i * STRIP, STRIP)
                x = recvb[c, s, pl.ds(r0, STRIP), :].astype(F32)
                turned = [x] + [pltpu.roll(x, 32 * d, 1) for d in (1, 2, 3)]
                for k in range(4):
                    spread = turned[(3 - k) % 4]
                    for b in range(3):
                        spread = jnp.where(quad == b, turned[(b - k) % 4], spread)
                    spread = spread.astype(BF16)
                    at_rows = pl.ds(pl.multiple_of(k * 256 + r0, STRIP), STRIP)
                    for h in range(2):
                        cols = pl.ds(h * 128, 128)
                        wide[at_rows, cols] = spread * mask[s, at_rows, cols]
                return 0

            lax.fori_loop(0, 256 // STRIP, widen, 0)
            acc[...] += jnp.dot(onehot[s], wide[...], preferred_element_type=F32)
            return 0

        lax.fori_loop(0, 8, body, 0)

    def send_sums(c):
        zsend[c] = acc[...].astype(BF16)
        return start(remote(zsend.at[c], zrecv.at[c], z_send.at[c], z_recv.at[c], {Z: moved(Z, CHUNKS[c])}))

    group_sums(0)
    z_copies = [send_sums(0)]

    for copy in lz:
        copy.wait_recv()
    lsend[2] = lsend[1] + sum(lrz[k] for k in range(1, 8))
    ly = [start(remote(lsend.at[2], lry.at[k], l_send.at[2, k], l_recv.at[2, k], y_peers[k])) for k in range(1, 8)]
    send_pieces(3)
    for copy in g2:
        copy.wait_recv()
    g3 = [
        start(remote(gbuf.at[:, :, ci, quarter], gbuf.at[:, :, ci, quarter], g_send.at[2, o], g_recv.at[2, o], x_peers[o]))
        for o in range(3)
    ]

    group_sums(1)
    z_copies.append(send_sums(1))
    for copy in g3:
        copy.wait_recv()
    g4 = start(remote(gbuf.at[:, :, ci], gbuf.at[:, :, ci], g_send.at[3, 0], g_recv.at[3, 0], {CORE: 1 - ci}))

    group_sums(2)
    z_copies.append(send_sums(2))
    g4.wait_recv()
    geno_out = pltpu.make_async_copy(gbuf, geno_ref, out_sem)
    geno_out.start()

    for copy in ly:
        copy.wait_recv()
    library_parts = three_parts(jnp.maximum(lsend[2] + sum(lry[k] for k in range(1, 8)), 1.0))

    group_sums(3)
    for copy in z_copies:
        copy.wait_recv()
    type_row = lax.broadcasted_iota(jnp.int32, (32, 256), 0)
    tl = lax.broadcasted_iota(jnp.int32, (32, 256), 1) // 32
    for t in range(3):
        at_rows = pl.ds(t * 128, 128)
        expand = jnp.where(type_row == tl + 8 * t, 1.0, 0.0).astype(BF16)
        library = sum(lax.dot_general(part, expand, TN, preferred_element_type=F32) for part in library_parts)
        pseudo = acc[at_rows, :]
        for c in range(3):
            pseudo = pseudo + zrecv[c, at_rows, :].astype(F32)
        logged = jnp.log1p(10000.0 * pseudo / library)
        spread = logged - jnp.mean(logged, axis=0, keepdims=True)
        standard = spread * lax.rsqrt(jnp.mean(spread * spread, axis=0, keepdims=True) + 1e-06)
        std_ref[pl.ds(t * 256, 256), :] = jnp.transpose(standard).astype(BF16)
    geno_out.wait()
    for copy in pending:
        copy.wait_send()


def scores_kernel(std_ref, geno_ref, out_ref):
    geno = jnp.concatenate([geno_ref[i] for i in range(geno_ref.shape[0])], axis=1)
    product = jnp.dot(std_ref[...], geno, preferred_element_type=F32) * DONORS ** (-0.5)
    out_ref[...] = product.astype(BF16)


def on_device(umi_counts, cell_donors, cell_types, live_cells, dosages):
    vmem = pl.BlockSpec(memory_space=pltpu.VMEM)
    hbm = pl.BlockSpec(memory_space=pl.ANY)
    dma = pltpu.SemaphoreType.DMA
    standard, geno = pl.pallas_call(
        gather_kernel,
        name="gather",
        out_shape=(
            jax.ShapeDtypeStruct((768, 128), BF16),
            jax.ShapeDtypeStruct((4, 4, 2, 128, 128), BF16),
        ),
        in_specs=[pl.BlockSpec(memory_space=pltpu.SMEM), hbm, vmem, vmem, vmem],
        out_specs=(vmem, hbm),
        scratch_shapes=[
            pltpu.VMEM((4, 1024, 256), jnp.int32),
            pltpu.VMEM((4, 8, 256, 128), BF16),
            pltpu.VMEM((4, 8, 256, 128), BF16),
            pltpu.VMEM((8, 8, 128), jnp.int32),
            pltpu.VMEM((8, 384, 1024), BF16),
            pltpu.VMEM((8, 1024, 256), BF16),
            pltpu.VMEM((1024, 256), BF16),
            pltpu.VMEM((384, 256), F32),
            pltpu.VMEM((3, 384, 256), BF16),
            pltpu.VMEM((3, 384, 256), BF16),
            pltpu.VMEM((256, 128), F32),
            pltpu.VMEM((128, 128), BF16),
            pltpu.VMEM((4, 4, 2, 128, 128), BF16),
            pltpu.VMEM((3, 32, 128), F32),
            pltpu.VMEM((3, 32, 128), F32),
            pltpu.VMEM((8, 32, 128), F32),
            pltpu.VMEM((8, 32, 128), F32),
            dma((4,)), dma((4, 8)), dma((4, 8)), dma((8,)), dma((8,)), dma((4, 3)), dma((4, 3)),
            dma((3, 8)), dma((3, 8)), dma((3,)), dma((3,)), dma,
        ],
        compiler_params=pltpu.CompilerParams(
            collective_id=0, has_side_effects=True, vmem_limit_bytes=48 * 1024 * 1024
        ),
    )(live_cells, umi_counts, cell_donors.reshape(8, 128), cell_types.reshape(8, 128), dosages)
    geno = geno.reshape(32, 128, 128)
    scores = pl.pallas_call(
        scores_kernel,
        name="scores",
        grid=(8,),
        out_shape=jax.ShapeDtypeStruct((768, 4096), BF16),
        in_specs=[pl.BlockSpec((768, 128), lambda i: (0, 0)), pl.BlockSpec((4, 128, 128), lambda i: (i, 0, 0))],
        out_specs=pl.BlockSpec((768, 512), lambda i: (0, i)),
    )(standard, geno)
    return scores.reshape(TYPES, 32, 4096)


def solution(mesh):
    torus = Mesh(mesh.devices.reshape(*SIZES.values()), AXES)
    return jax.shard_map(
        on_device,
        mesh=torus,
        in_specs=(P(BATCH, GENE), P(BATCH), P(BATCH), P(BATCH), P(None, BATCH)),
        out_specs=P(None, GENE + BATCH, None),
        check_vma=False,
    )
```

time: 256 us -> 78.4 us (0.31); the launches traced: 252 us -> 78 us
  waiting for transfers between devices: 147 us -> 0 us
  Pallas kernels: 0 us -> 71.3 us
  blocking collectives: 57.4 us -> 0 us
  matrix products: 17.7 us -> 0 us
  between operations: 15.6 us -> 0.68 us
  local copies, waits for them, and re-layouts: 10.9 us -> 6.03 us
  other arithmetic: 3.33 us -> 0 us
    reduce_scatter x2 -> x0, waiting for transfers between devices: 147 us -> none  [the longest x1 116 us: summed_rows_2(): return lax.psum_scatter(tiles, chips, scatter_dimension=0, tiled=True)[0]]
    pallas_call x0 -> x2, Pallas kernels: none -> 71.3 us  [the longest x1 63.9 us: on_device(): pl.pallas_call(gather_kernel, name='gather', out_shape=(jax.ShapeDtypeStr...]
    psum x5 -> x0, blocking collectives: 57.4 us -> none  [one_axis_at_a_time(): value = lax.psum(value, axis)]
    dot_general x2 -> x0, matrix products: 17.7 us -> none  [the longest x1 12 us: on_device(): lax.dot_general(rounded, table, (((0,), (0,)), ((), ())), preferred_eleme...]
    another operation x1 -> x0, local copies, waits for them, and re-layouts: 10.8 us -> none  [summed_rows_2(): tiles = tiles.reshape(*sizes, *inside).swapaxes(0, 1).reshape(-1, *inside)]
    unnamed x3 -> x12, local copies, waits for them, and re-layouts: 0.08 us -> 6.03 us
  transfers between devices with their start and end apart: 3 -> 0, of which waited for: 2 -> 0; matrix products, arithmetic and copies ran while one was open for 1% -> 0% of each run, Pallas kernels for 0% -> 0%
where the time goes in v1:
time: 78.4 us; the launch traced here: 78 us
  Pallas kernels  71.3 us (91%)
  local copies, waits for them, and re-layouts  6.03 us (8%)
    pallas_call x1, Pallas kernels, on_device(): pl.pallas_call(gather_kernel, name='gather', out_shape=(jax.ShapeDtypeStr...  63.9 us
    pallas_call x1, Pallas kernels, on_device(): pl.pallas_call(scores_kernel, name='scores', grid=(8,), out_shape=jax.Sha...  7.35 us
    unnamed x12, local copies, waits for them, and re-layouts  6.03 us

profile of v1, /device:TPU:1, one launch (start us, length us, event | category | flops | bytes accessed | tf_op | source)
XLA Modules:
  0.0 78.0 jit_solution(4693878934778913011)
XLA Ops:
  0.7 0.0 copy-start
  0.7 2.2 %copy-done = s32[1024,1024]{1,0:T(8,128)S(1)} copy-done((s32[1024,1024]{1,0:T(8,128)S(1)}, s32[1024,1024]{1,0:T(8,128)}, u32[]{:S(2)}) %copy-start) | copy-done | bytes 4194328
  2.8 0.0 copy-start.3
  2.8 0.8 %copy-done.3 = s32[128,128]{1,0:T(8,128)S(1)} copy-done((s32[128,128]{1,0:T(8,128)S(1)}, s32[128,128]{1,0:T(8,128)}, u32[]{:S(2)}) %copy-start.3) | copy-done | bytes 65560
  3.7 0.0 copy-start.4
  3.7 0.7 copy-done.4
  4.4 0.0 copy-start.5
  4.4 0.7 copy-done.5
  5.1 63.9 %gather.1 = (bf16[768,128]{1,0:T(8,128)(2,1)S(1)}, bf16[4,4,2,128,128]{4,3,2,1,0:T(8,128)(2,1)S(1)}) custom-call(s32[1]{0:T(128)S(6)} %copy.6.live_ref, s32[1024,1024]{1,0:T(8,128)S(1)} %copy-done, s32[8,128]{1,0:T(8,128)S(1)} %bitcast.5, s32[8,128]{1,0:T(8,128)S(1)} %bitcast.6, s32[128,128]{1,0:T(8,128)S(1)} %copy-done.3), custom_call_target="tpu_custom_call" | custom-call | tf_op jit(solution)/shard_map/gather/pallas_call | solution.py:292
  69.0 0.0 copy-start.1
  69.0 1.0 %copy-done.1 = bf16[4,4,2,128,128]{4,3,2,1,0:T(8,128)(2,1)} copy-done((bf16[4,4,2,128,128]{4,3,2,1,0:T(8,128)(2,1)}, bf16[4,4,2,128,128]{4,3,2,1,0:T(8,128)(2,1)S(1)}, u32[]{:S(2)}) %copy-start.1) | copy-done | bytes 1048600
  70.0 0.0 copy-start.2
  70.0 0.7 copy-done.2
  70.7 7.3 %scores.1 = bf16[768,4096]{1,0:T(8,128)(2,1)} custom-call(bf16[768,128]{1,0:T(8,128)(2,1)} %copy-done.2, bf16[32,128,128]{2,1,0:T(8,128)(2,1)} %bitcast.4), custom_call_target="tpu_custom_call" | custom-call | tf_op jit(solution)/shard_map/scores/pallas_call | solution.py:327
Async XLA Ops:
  0.7 2.2 %copy-start = (s32[1024,1024]{1,0:T(8,128)S(1)}, s32[1024,1024]{1,0:T(8,128)}, u32[]{:S(2)}) copy-start(s32[1024,1024]{1,0:T(8,128)} %umi_ref.1) | copy-start | bytes 12582916
  2.8 0.8 %copy-start.3 = (s32[128,128]{1,0:T(8,128)S(1)}, s32[128,128]{1,0:T(8,128)}, u32[]{:S(2)}) copy-start(s32[128,128]{1,0:T(8,128)} %dosages_ref.1) | copy-start | bytes 196612
  3.7 0.7 copy-start.4
  4.4 0.7 copy-start.5
  69.0 1.0 %copy-start.1 = (bf16[4,4,2,128,128]{4,3,2,1,0:T(8,128)(2,1)}, bf16[4,4,2,128,128]{4,3,2,1,0:T(8,128)(2,1)S(1)}, u32[]{:S(2)}) copy-start(bf16[4,4,2,128,128]{4,3,2,1,0:T(8,128)(2,1)S(1)} %get-tuple-element.8) | copy-start | bytes 3145732
  70.0 0.7 copy-start.2

commit v2 on v1

--- a/solution.py
+++ b/solution.py
@@ -17,11 +17,15 @@
 F32 = jnp.float32
 BF16 = jnp.bfloat16
 
-CHUNKS = (2, 1, 3, 0)
+BLOCKS = (2, 1, 3, 0)
+CODE = 2112.0
+LOG2 = 0.6931471805599453
 SLOTS = tuple((dy, dc) for dy in (0, 1, 3, 2) for dc in (0, 1))
 ZSLOTS = tuple((oz, ol) for oz in range(4) for ol in range(2))
 OFFS = (1, 2, 3)
-STRIP = 32
+STRIP = 128
+COLUMNS = 1024
+VMEM_LIMIT = 67043328
 NT = (((1,), (1,)), ((), ()))
 TN = (((0,), (0,)), ((), ()))
 
@@ -34,10 +38,18 @@
     return first, second, third
 
 
+def coded(sums):
+    return ((jnp.log(1.0 + sums) * (CODE / LOG2) + 0.5).astype(jnp.int32) - 32768).astype(jnp.int16)
+
+
+def decoded(codes):
+    return jnp.exp((codes.astype(jnp.int32) + 32768).astype(F32) * (LOG2 / CODE)) - 1.0
+
+
 def gather_kernel(
     live_ref, umi_ref, donors_ref, types_ref, dosages_ref,
     std_ref, geno_ref,
-    xin, sendb, recvb, codeb, onehot, mask, wide, acc, zsend, zrecv, rows, gown, gbuf, lsend, lrx, lrz, lry,
+    xin, sendb, recvb, codeb, onehot, mask, acc, zsend, zrecv, rows, gown, gbuf, lsend, lrx, lrz, lry,
     in_sem, d_send, d_recv, c_send, c_recv, g_send, g_recv, l_send, l_recv, z_send, z_recv, out_sem,
 ):
     at = {axis: lax.axis_index(axis) for axis in AXES}
@@ -59,11 +71,10 @@
     x_peers = [peer(gene_0=o) for o in OFFS]
 
     loads = []
-    for c, off in enumerate(CHUNKS):
+    for c, off in enumerate(BLOCKS):
         col = pl.multiple_of(moved(Z, off) * 256, 256)
-        load = pltpu.make_async_copy(umi_ref.at[:, pl.ds(col, 256)], xin.at[c], in_sem.at[c])
-        load.start()
-        loads.append(load)
+        loads.append(pltpu.make_async_copy(umi_ref.at[:, pl.ds(col, 256)], xin.at[c], in_sem.at[c]))
+    loads[0].start()
 
     barrier = pltpu.get_barrier_semaphore()
     for device in y_peers[1:] + z_peers[1:] + x_peers:
@@ -84,16 +95,20 @@
     lane = lax.broadcasted_iota(jnp.int32, (STRIP, 128), 1)
     low = lane < 64
     even = (lane & 32) == 0
+    first = (lane & 16) == 0
 
     def pack(c):
         def body(i, _):
             r0 = pl.multiple_of(i * STRIP, STRIP)
             total = None
             for h in range(2):
-                x = [
-                    xin[c, pl.ds(pl.multiple_of(k * 256 + r0, STRIP), STRIP), pl.ds(h * 128, 128)].astype(F32)
-                    for k in range(4)
-                ]
+                x = []
+                for k in range(4):
+                    cells = pl.ds(pl.multiple_of(k * 256 + r0, STRIP), STRIP)
+                    value = xin[c, cells, pl.ds(h * 128, 128)]
+                    if c in (1, 2):
+                        value = jnp.where(first, value, xin[3 - c, cells, pl.ds(h * 128, 128)])
+                    x.append(value.astype(F32))
                 a = [None] * 4
                 for k in range(2):
                     a[k] = jnp.where(low, x[k], pltpu.roll(x[k + 2], 64, 1))
@@ -127,22 +142,25 @@
             start(remote(sendb.at[c, piece], recvb.at[c, k], d_send.at[c, k], d_recv.at[c, k], y_peers[k]))
 
     loads[0].wait()
+    for c in (1, 2, 3):
+        loads[c].start()
     pack(0)
     pl.semaphore_wait(barrier, 7 + 7 + 3)
-    send_pieces(0)
     code_copies = [
         start(remote(codeb.at[0], codeb.at[k], c_send.at[k], c_recv.at[k], y_peers[k])) for k in range(1, 8)
     ]
+    send_pieces(0)
     g1 = [
         start(remote(gbuf.at[zi, yi, ci, quarter], gbuf.at[zi, yi, ci, quarter], g_send.at[0, o], g_recv.at[0, o], {Z: moved(Z, off)}))
         for o, off in enumerate(OFFS)
     ]
     loads[1].wait()
+    loads[2].wait()
     pack(1)
     send_pieces(1)
-    for c in (2, 3):
-        loads[c].wait()
-        pack(c)
+    pack(2)
+    loads[3].wait()
+    pack(3)
     for c in range(4):
         recvb[c, 0] = sendb[c, own]
 
@@ -163,36 +181,44 @@
     lsend[0] = part_library
     lx = [start(remote(lsend.at[0], lrx.at[o], l_send.at[0, o], l_recv.at[0, o], x_peers[o])) for o in range(3)]
 
-    block = lax.broadcasted_iota(jnp.int32, (128, 128), 1) // 32
+    block = (lax.broadcasted_iota(jnp.int32, (128, 128), 1) // 32).astype(F32).astype(BF16)
+    donor_at = lax.broadcasted_iota(jnp.int32, (128, 128), 0).astype(F32).astype(BF16)
+    one, zero = jnp.ones((128, 128), BF16), jnp.zeros((128, 128), BF16)
+
+    def down(row):
+        return jnp.concatenate([jnp.broadcast_to(row, (16, 128)).astype(BF16)] * 8, axis=0)
 
     def build(s):
         code = codeb[s]
-        columns = jnp.transpose((code & 7).astype(F32)).astype(jnp.int32)
-        group = code >> 3
+        columns = jnp.transpose((code & 7).astype(F32))
+        donor = ((code >> 3) & 127).astype(F32)
+        high = [jnp.where((code >> 10) == t, 1.0, 0.0) for t in range(3)]
         for g in range(8):
-            match = lax.broadcasted_iota(jnp.int32, (384, 128), 0) == group[g : g + 1, :]
-            onehot[s, :, pl.ds(g * 128, 128)] = jnp.where(match, 1.0, 0.0).astype(BF16)
-            column = columns[:, g : g + 1]
+            cells = pl.ds(g * 128, 128)
+            match = donor_at == down(donor[g : g + 1, :])
+            for t in range(3):
+                onehot[s, pl.ds(t * 128, 128), cells] = jnp.where(match, down(high[t][g : g + 1, :]), zero)
+            column = jnp.broadcast_to(columns[:, g : g + 1], (128, 128)).astype(BF16)
             for h in range(2):
-                mask[s, pl.ds(g * 128, 128), pl.ds(h * 128, 128)] = jnp.where(column == block + 4 * h, 1.0, 0.0).astype(BF16)
+                mask[s, cells, pl.ds(h * 128, 128)] = jnp.where(column == block + 4 * h, one, zero)
 
     build(0)
+    for copy in code_copies:
+        copy.wait_recv()
+    lax.fori_loop(1, 8, lambda s, _: (build(s), 0)[1], 0)
     for copy in g1:
         copy.wait_recv()
     g2 = [
         start(remote(gbuf.at[:, yi, ci, quarter], gbuf.at[:, yi, ci, quarter], g_send.at[1, o], g_recv.at[1, o], {Y: moved(Y, off)}))
         for o, off in enumerate(OFFS)
     ]
-    for copy in code_copies:
-        copy.wait_recv()
-    lax.fori_loop(1, 8, lambda s, _: (build(s), 0)[1], 0)
     send_pieces(2)
     for copy in lx:
         copy.wait_recv()
     lsend[1] = lsend[0] + lrx[0] + lrx[1] + lrx[2]
     lz = [start(remote(lsend.at[1], lrz.at[k], l_send.at[1, k], l_recv.at[1, k], z_peers[k])) for k in range(1, 8)]
 
-    quad = lax.broadcasted_iota(jnp.int32, (STRIP, 128), 1) // 32
+    quad = (lax.broadcasted_iota(jnp.int32, (256, 128), 1) // 32).astype(F32).astype(BF16)
 
     def group_sums(c):
         acc[...] = jnp.zeros_like(acc)
@@ -202,34 +228,45 @@
             def _():
                 remote(recvb.at[c, s], recvb.at[c, s], d_send.at[c, s], d_recv.at[c, s], y_peers[1]).wait_recv()
 
-            def widen(i, _):
-                r0 = pl.multiple_of(i * STRIP, STRIP)
-                x = recvb[c, s, pl.ds(r0, STRIP), :].astype(F32)
-                turned = [x] + [pltpu.roll(x, 32 * d, 1) for d in (1, 2, 3)]
-                for k in range(4):
-                    spread = turned[(3 - k) % 4]
-                    for b in range(3):
-                        spread = jnp.where(quad == b, turned[(b - k) % 4], spread)
-                    spread = spread.astype(BF16)
-                    at_rows = pl.ds(pl.multiple_of(k * 256 + r0, STRIP), STRIP)
-                    for h in range(2):
-                        cols = pl.ds(h * 128, 128)
-                        wide[at_rows, cols] = spread * mask[s, at_rows, cols]
-                return 0
-
-            lax.fori_loop(0, 256 // STRIP, widen, 0)
-            acc[...] += jnp.dot(onehot[s], wide[...], preferred_element_type=F32)
+            piece = recvb[c, s]
+            x = piece.astype(F32)
+            turned = [piece] + [pltpu.roll(x, 32 * d, 1).astype(BF16) for d in (1, 2, 3)]
+            wide = []
+            for k in range(4):
+                spread = turned[(3 - k) % 4]
+                for b in range(3):
+                    spread = jnp.where(quad == b, turned[(b - k) % 4], spread)
+                at_rows = pl.ds(k * 256, 256)
+                wide.append(jnp.concatenate([spread * mask[s, at_rows, pl.ds(h * 128, 128)] for h in range(2)], axis=1))
+            acc[...] += jnp.dot(onehot[s], jnp.concatenate(wide, axis=0), preferred_element_type=F32)
             return 0
 
         lax.fori_loop(0, 8, body, 0)
 
+    near = (lax.broadcasted_iota(jnp.int32, (384, 128), 1) & 16) == 0
+
     def send_sums(c):
-        zsend[c] = acc[...].astype(BF16)
-        return start(remote(zsend.at[c], zrecv.at[c], z_send.at[c], z_recv.at[c], {Z: moved(Z, CHUNKS[c])}))
-
+        lower, upper = acc[:, pl.ds(0, 128)], acc[:, pl.ds(128, 128)]
+        a = jnp.where(near, lower, pltpu.roll(upper, 16, 1))
+        b = jnp.where(near, pltpu.roll(lower, 112, 1), upper)
+        up, down_ = (a, b) if c == 1 else (b, a)
+        if c == 2:
+            for copy in z_copies[:2]:
+                copy.wait_recv()
+            up, down_ = up + decoded(zrecv[0, 0]), down_ + decoded(zrecv[0, 1])
+        zsend[c, 0] = coded(up)
+        zsend[c, 1] = coded(down_)
+        for d, off in enumerate((1, 3)):
+            z_copies.append(
+                start(remote(zsend.at[c, d], zrecv.at[c, d], z_send.at[c, d], z_recv.at[c, d], {Z: moved(Z, off)}))
+            )
+
+    z_copies = []
     group_sums(0)
-    z_copies = [send_sums(0)]
-
+    send_sums(0)
+
+    group_sums(1)
+    send_sums(1)
     for copy in lz:
         copy.wait_recv()
     lsend[2] = lsend[1] + sum(lrz[k] for k in range(1, 8))
@@ -242,34 +279,32 @@
         for o in range(3)
     ]
 
-    group_sums(1)
-    z_copies.append(send_sums(1))
+    group_sums(2)
+    send_sums(2)
+
+    group_sums(3)
     for copy in g3:
         copy.wait_recv()
     g4 = start(remote(gbuf.at[:, :, ci], gbuf.at[:, :, ci], g_send.at[3, 0], g_recv.at[3, 0], {CORE: 1 - ci}))
-
-    group_sums(2)
-    z_copies.append(send_sums(2))
+    for copy in ly:
+        copy.wait_recv()
+    library_parts = three_parts(jnp.maximum(lsend[2] + sum(lry[k] for k in range(1, 8)), 1.0))
     g4.wait_recv()
     geno_out = pltpu.make_async_copy(gbuf, geno_ref, out_sem)
     geno_out.start()
-
-    for copy in ly:
-        copy.wait_recv()
-    library_parts = three_parts(jnp.maximum(lsend[2] + sum(lry[k] for k in range(1, 8)), 1.0))
-
-    group_sums(3)
-    for copy in z_copies:
+    for copy in z_copies[2:]:
         copy.wait_recv()
     type_row = lax.broadcasted_iota(jnp.int32, (32, 256), 0)
     tl = lax.broadcasted_iota(jnp.int32, (32, 256), 1) // 32
+    here = near[:128]
     for t in range(3):
         at_rows = pl.ds(t * 128, 128)
         expand = jnp.where(type_row == tl + 8 * t, 1.0, 0.0).astype(BF16)
         library = sum(lax.dot_general(part, expand, TN, preferred_element_type=F32) for part in library_parts)
-        pseudo = acc[at_rows, :]
-        for c in range(3):
-            pseudo = pseudo + zrecv[c, at_rows, :].astype(F32)
+        a = decoded(zrecv[1, 0, at_rows, :]) + decoded(zrecv[2, 1, at_rows, :])
+        b = decoded(zrecv[2, 0, at_rows, :]) + decoded(zrecv[1, 1, at_rows, :])
+        others = [jnp.where(here, a, pltpu.roll(b, 16, 1)), jnp.where(here, pltpu.roll(a, 112, 1), b)]
+        pseudo = acc[at_rows, :] + jnp.concatenate(others, axis=1)
         logged = jnp.log1p(10000.0 * pseudo / library)
         spread = logged - jnp.mean(logged, axis=0, keepdims=True)
         standard = spread * lax.rsqrt(jnp.mean(spread * spread, axis=0, keepdims=True) + 1e-06)
@@ -279,10 +314,22 @@
         copy.wait_send()
 
 
-def scores_kernel(std_ref, geno_ref, out_ref):
-    geno = jnp.concatenate([geno_ref[i] for i in range(geno_ref.shape[0])], axis=1)
-    product = jnp.dot(std_ref[...], geno, preferred_element_type=F32) * DONORS ** (-0.5)
-    out_ref[...] = product.astype(BF16)
+def scores_kernel(std_ref, geno_ref, out_ref, buffer, sem):
+    def store(i):
+        columns = pl.ds(pl.multiple_of(i * COLUMNS, COLUMNS), COLUMNS)
+        return pltpu.make_async_copy(buffer.at[i], out_ref.at[:, columns], sem.at[i])
+
+    def body(i, _):
+        count = COLUMNS // 128
+        geno = jnp.concatenate([geno_ref[i * count + j] for j in range(count)], axis=1)
+        product = jnp.dot(std_ref[...], geno, preferred_element_type=F32) * DONORS ** (-0.5)
+        buffer[i] = product.astype(BF16)
+        store(i).start()
+        return 0
+
+    steps = buffer.shape[0]
+    lax.fori_loop(0, steps, body, 0)
+    lax.fori_loop(0, steps, lambda i, _: (store(i).wait(), 0)[1], 0)
 
 
 def on_device(umi_counts, cell_donors, cell_types, live_cells, dosages):
@@ -305,10 +352,9 @@
             pltpu.VMEM((8, 8, 128), jnp.int32),
             pltpu.VMEM((8, 384, 1024), BF16),
             pltpu.VMEM((8, 1024, 256), BF16),
-            pltpu.VMEM((1024, 256), BF16),
             pltpu.VMEM((384, 256), F32),
-            pltpu.VMEM((3, 384, 256), BF16),
-            pltpu.VMEM((3, 384, 256), BF16),
+            pltpu.VMEM((3, 2, 384, 128), jnp.int16),
+            pltpu.VMEM((3, 2, 384, 128), jnp.int16),
             pltpu.VMEM((256, 128), F32),
             pltpu.VMEM((128, 128), BF16),
             pltpu.VMEM((4, 4, 2, 128, 128), BF16),
@@ -317,20 +363,21 @@
             pltpu.VMEM((8, 32, 128), F32),
             pltpu.VMEM((8, 32, 128), F32),
             dma((4,)), dma((4, 8)), dma((4, 8)), dma((8,)), dma((8,)), dma((4, 3)), dma((4, 3)),
-            dma((3, 8)), dma((3, 8)), dma((3,)), dma((3,)), dma,
+            dma((3, 8)), dma((3, 8)), dma((3, 2)), dma((3, 2)), dma,
         ],
         compiler_params=pltpu.CompilerParams(
-            collective_id=0, has_side_effects=True, vmem_limit_bytes=48 * 1024 * 1024
+            collective_id=0, has_side_effects=True, vmem_limit_bytes=VMEM_LIMIT
         ),
     )(live_cells, umi_counts, cell_donors.reshape(8, 128), cell_types.reshape(8, 128), dosages)
     geno = geno.reshape(32, 128, 128)
     scores = pl.pallas_call(
         scores_kernel,
         name="scores",
-        grid=(8,),
         out_shape=jax.ShapeDtypeStruct((768, 4096), BF16),
-        in_specs=[pl.BlockSpec((768, 128), lambda i: (0, 0)), pl.BlockSpec((4, 128, 128), lambda i: (i, 0, 0))],
-        out_specs=pl.BlockSpec((768, 512), lambda i: (0, i)),
+        in_specs=[vmem, vmem],
+        out_specs=hbm,
+        scratch_shapes=[pltpu.VMEM((4096 // COLUMNS, 768, COLUMNS), BF16), dma((4096 // COLUMNS,))],
+        compiler_params=pltpu.CompilerParams(vmem_limit_bytes=VMEM_LIMIT),
     )(standard, geno)
     return scores.reshape(TYPES, 32, 4096)
 

time: 78.4 us -> 49.5 us (0.63)
  Pallas kernels: 71.3 us -> 48.6 us
  local copies, waits for them, and re-layouts: 6.03 us -> 0 us
    pallas_call x1, Pallas kernels: 63.9 us -> 43.8 us  [on_device(): pl.pallas_call(gather_kernel, name='gather', out_shape=(jax.ShapeDtypeStr...]
    unnamed x12 -> x0, local copies, waits for them, and re-layouts: 6.03 us -> none
    pallas_call x1, Pallas kernels: 7.35 us -> 4.76 us  [on_device(): pl.pallas_call(scores_kernel, name='scores', out_shape=jax.ShapeDtypeStru...]
where the time goes in v2:
time: 49.5 us; the launch traced here: 49.3 us
  Pallas kernels  48.6 us (98%)
  between operations  0.66 us (1%)
    pallas_call x1, Pallas kernels, on_device(): pl.pallas_call(gather_kernel, name='gather', out_shape=(jax.ShapeDtypeStr...  43.8 us
    pallas_call x1, Pallas kernels, on_device(): pl.pallas_call(scores_kernel, name='scores', out_shape=jax.ShapeDtypeStru...  4.76 us

profile of v2, /device:TPU:1, one launch (start us, length us, event | category | flops | bytes accessed | tf_op | source)
XLA Modules:
  0.0 49.3 jit_solution(12352318350900652751)
XLA Ops:
  0.7 43.8 %gather.1 = (bf16[768,128]{1,0:T(8,128)(2,1)}, bf16[4,4,2,128,128]{4,3,2,1,0:T(8,128)(2,1)}) custom-call(s32[1]{0:T(128)S(6)} %copy.6.live_ref, s32[1024,1024]{1,0:T(8,128)} %umi_ref.1, s32[8,128]{1,0:T(8,128)} %bitcast.5, s32[8,128]{1,0:T(8,128)} %bitcast.6, s32[128,128]{1,0:T(8,128)} %dosages_ref.1), custom_call_target="tpu_custom_call" | custom-call | tf_op jit(solution)/shard_map/gather/pallas_call | solution.py:339
  44.5 4.8 %scores.1 = bf16[768,4096]{1,0:T(8,128)(2,1)} custom-call(bf16[768,128]{1,0:T(8,128)(2,1)} %get-tuple-element.7.std_ref, bf16[32,128,128]{2,1,0:T(8,128)(2,1)} %bitcast.4), custom_call_target="tpu_custom_call" | custom-call | tf_op jit(solution)/shard_map/scores/pallas_call | solution.py:373

commit v3 on v2

--- a/solution.py
+++ b/solution.py
@@ -20,11 +20,11 @@
 BLOCKS = (2, 1, 3, 0)
 CODE = 2112.0
 LOG2 = 0.6931471805599453
-SLOTS = tuple((dy, dc) for dy in (0, 1, 3, 2) for dc in (0, 1))
+SLOTS = tuple((dy, dc) for dy in (0, 2, 1, 3) for dc in (0, 1))
 ZSLOTS = tuple((oz, ol) for oz in range(4) for ol in range(2))
 OFFS = (1, 2, 3)
 STRIP = 128
-COLUMNS = 1024
+BANDS = (512, 512, 1024, 1024, 1024)
 VMEM_LIMIT = 67043328
 NT = (((1,), (1,)), ((), ()))
 TN = (((0,), (0,)), ((), ()))
@@ -47,10 +47,11 @@
 
 
 def gather_kernel(
-    live_ref, umi_ref, donors_ref, types_ref, dosages_ref,
+    live_ref, umi_ref, donors_hbm, types_hbm, dosages_hbm,
     std_ref, geno_ref,
-    xin, sendb, recvb, codeb, onehot, mask, acc, zsend, zrecv, rows, gown, gbuf, lsend, lrx, lrz, lry,
-    in_sem, d_send, d_recv, c_send, c_recv, g_send, g_recv, l_send, l_recv, z_send, z_recv, out_sem,
+    donors_ref, types_ref, dosages_ref, std,
+    xin, sendb, recvb, codeb, onehot, mask, acc, zsend, zrecv, rows, gown, gbuf, lsend, lrx, lrc, lrz, lry, half_lib, library,
+    in_sem, d_send, d_recv, c_send, c_recv, g_send, g_recv, l_send, l_recv, z_send, z_recv, small_sem, out_sem,
 ):
     at = {axis: lax.axis_index(axis) for axis in AXES}
     zi, yi, ci, xi = at[Z], at[Y], at[CORE], at[X]
@@ -70,34 +71,40 @@
     z_peers = [peer(batch_0=oz, gene_1=ol) for oz, ol in ZSLOTS]
     x_peers = [peer(gene_0=o) for o in OFFS]
 
+    def cells_of(block):
+        return pl.ds(pl.multiple_of(block * 128, 128), 128)
+
+    smalls = [
+        pltpu.make_async_copy(src, dst, small_sem.at[i])
+        for i, (src, dst) in enumerate(
+            ((donors_hbm, donors_ref), (types_hbm, types_ref), (dosages_hbm, dosages_ref))
+        )
+    ]
+    for copy in smalls:
+        copy.start()
     loads = []
-    for c, off in enumerate(BLOCKS):
-        col = pl.multiple_of(moved(Z, off) * 256, 256)
-        loads.append(pltpu.make_async_copy(umi_ref.at[:, pl.ds(col, 256)], xin.at[c], in_sem.at[c]))
-    loads[0].start()
+    col = pl.ds(pl.multiple_of(moved(Z, BLOCKS[0]) * 256, 256), 256)
+    for i in range(2):
+        for k in range(4):
+            block = cells_of(2 * k + i)
+            loads.append(pltpu.make_async_copy(umi_ref.at[block, col], xin.at[0, block], in_sem.at[4 * i + k]))
+    for c in (1, 2, 3):
+        col = pl.ds(pl.multiple_of(moved(Z, BLOCKS[c]) * 256, 256), 256)
+        loads.append(pltpu.make_async_copy(umi_ref.at[:, col], xin.at[c], in_sem.at[7 + c]))
+    for load in loads[:8]:
+        load.start()
 
     barrier = pltpu.get_barrier_semaphore()
     for device in y_peers[1:] + z_peers[1:] + x_peers:
         pl.semaphore_signal(barrier, inc=1, device_id=device, device_id_type=MESH)
 
-    slot = lax.broadcasted_iota(jnp.int32, (8, 128), 0) * 128 + lax.broadcasted_iota(jnp.int32, (8, 128), 1)
-    alive = slot < live_ref[0]
-    types = types_ref[...]
-    donors = donors_ref[...]
-    codeb[0] = jnp.where(alive, ((types >> 3) * DONORS + donors) * 8 + (types & 7), -8)
-
-    genotype = dosages_ref[...].astype(F32)
-    centred = genotype - jnp.mean(genotype, axis=0, keepdims=True)
-    gown[...] = (centred * lax.rsqrt(jnp.mean(centred * centred, axis=0, keepdims=True) + 1e-06)).astype(BF16)
-    quarter = pl.ds(pl.multiple_of(xi * 32, 32), 32)
-    gbuf[zi, yi, ci, quarter, :] = gown[quarter, :]
     rows[...] = jnp.zeros_like(rows)
     lane = lax.broadcasted_iota(jnp.int32, (STRIP, 128), 1)
     low = lane < 64
     even = (lane & 32) == 0
     first = (lane & 16) == 0
 
-    def pack(c):
+    def pack(c, begin=0, end=2):
         def body(i, _):
             r0 = pl.multiple_of(i * STRIP, STRIP)
             total = None
@@ -125,7 +132,7 @@
             rows[pl.ds(r0, STRIP), :] += total
             return 0
 
-        lax.fori_loop(0, 256 // STRIP, body, 0)
+        lax.fori_loop(begin, end, body, 0)
 
     own = yi * 2 + ci
     pending = []
@@ -141,25 +148,53 @@
             piece = moved(Y, dy) * 2 + moved(CORE, dc)
             start(remote(sendb.at[c, piece], recvb.at[c, k], d_send.at[c, k], d_recv.at[c, k], y_peers[k]))
 
-    loads[0].wait()
-    for c in (1, 2, 3):
-        loads[c].start()
-    pack(0)
+    def send_half(i):
+        at_rows = pl.ds(i * 128, 128)
+        for k in (2, 3, 4, 5, 6, 7, 1):
+            dy, dc = SLOTS[k]
+            piece = moved(Y, dy) * 2 + moved(CORE, dc)
+            start(
+                remote(sendb.at[0, piece, at_rows], recvb.at[0, k, at_rows], d_send.at[4 * i, k], d_recv.at[4 * i, k], y_peers[k])
+            )
+
+    for load in loads[:4]:
+        load.wait()
+    for load in loads[8:]:
+        load.start()
+    pack(0, 0, 1)
+    for copy in smalls:
+        copy.wait()
+    slot = lax.broadcasted_iota(jnp.int32, (8, 128), 0) * 128 + lax.broadcasted_iota(jnp.int32, (8, 128), 1)
+    alive = slot < live_ref[0]
+    types = types_ref[...]
+    donors = donors_ref[...]
+    codeb[0] = jnp.where(alive, ((types >> 3) * DONORS + donors) * 8 + (types & 7), -8)
+
+    genotype = dosages_ref[...].astype(F32)
+    centred = genotype - jnp.mean(genotype, axis=0, keepdims=True)
+    gown[...] = (centred * lax.rsqrt(jnp.mean(centred * centred, axis=0, keepdims=True) + 1e-06)).astype(BF16)
+    quarter = pl.ds(pl.multiple_of(xi * 32, 32), 32)
+    gbuf[zi, yi, ci, quarter, :] = gown[quarter, :]
     pl.semaphore_wait(barrier, 7 + 7 + 3)
     code_copies = [
         start(remote(codeb.at[0], codeb.at[k], c_send.at[k], c_recv.at[k], y_peers[k])) for k in range(1, 8)
     ]
-    send_pieces(0)
     g1 = [
-        start(remote(gbuf.at[zi, yi, ci, quarter], gbuf.at[zi, yi, ci, quarter], g_send.at[0, o], g_recv.at[0, o], {Z: moved(Z, off)}))
+        start(remote(gbuf.at[zi, yi, ci, quarter], gbuf.at[zi, yi, ci, quarter], g_send.at[0, o], g_recv.at[0, o], {Y: moved(Y, off)}))
         for o, off in enumerate(OFFS)
     ]
-    loads[1].wait()
-    loads[2].wait()
+    send_half(0)
+    for load in loads[4:8]:
+        load.wait()
+    pack(0, 1, 2)
+    send_half(1)
+    loads[8].wait()
+    loads[9].wait()
     pack(1)
     send_pieces(1)
     pack(2)
-    loads[3].wait()
+    send_pieces(2)
+    loads[10].wait()
     pack(3)
     for c in range(4):
         recvb[c, 0] = sendb[c, own]
@@ -203,30 +238,36 @@
                 mask[s, cells, pl.ds(h * 128, 128)] = jnp.where(column == block + 4 * h, one, zero)
 
     build(0)
+    for copy in g1:
+        copy.wait_recv()
+    g2 = [
+        start(remote(gbuf.at[zi, :, ci, quarter], gbuf.at[zi, :, ci, quarter], g_send.at[1, o], g_recv.at[1, o], {Z: moved(Z, off)}))
+        for o, off in enumerate(OFFS)
+    ]
     for copy in code_copies:
         copy.wait_recv()
     lax.fori_loop(1, 8, lambda s, _: (build(s), 0)[1], 0)
-    for copy in g1:
-        copy.wait_recv()
-    g2 = [
-        start(remote(gbuf.at[:, yi, ci, quarter], gbuf.at[:, yi, ci, quarter], g_send.at[1, o], g_recv.at[1, o], {Y: moved(Y, off)}))
-        for o, off in enumerate(OFFS)
-    ]
-    send_pieces(2)
     for copy in lx:
         copy.wait_recv()
     lsend[1] = lsend[0] + lrx[0] + lrx[1] + lrx[2]
-    lz = [start(remote(lsend.at[1], lrz.at[k], l_send.at[1, k], l_recv.at[1, k], z_peers[k])) for k in range(1, 8)]
+    lc = start(remote(lsend.at[1], lrc, l_send.at[0, 3], l_recv.at[0, 3], {CORE: 1 - ci}))
+    half = pl.ds(pl.multiple_of(ci * 16, 16), 16)
 
     quad = (lax.broadcasted_iota(jnp.int32, (256, 128), 1) // 32).astype(F32).astype(BF16)
 
-    def group_sums(c):
-        acc[...] = jnp.zeros_like(acc)
+    def group_sums(c, begin=0, end=8):
+        if begin == 0:
+            acc[...] = jnp.zeros_like(acc)
 
         def body(s, _):
             @pl.when(s > 0)
             def _():
-                remote(recvb.at[c, s], recvb.at[c, s], d_send.at[c, s], d_recv.at[c, s], y_peers[1]).wait_recv()
+                if c == 0:
+                    for i in range(2):
+                        part = recvb.at[0, s, pl.ds(i * 128, 128)]
+                        remote(part, part, d_send.at[4 * i, s], d_recv.at[4 * i, s], y_peers[1]).wait_recv()
+                else:
+                    remote(recvb.at[c, s], recvb.at[c, s], d_send.at[c, s], d_recv.at[c, s], y_peers[1]).wait_recv()
 
             piece = recvb[c, s]
             x = piece.astype(F32)
@@ -241,7 +282,7 @@
             acc[...] += jnp.dot(onehot[s], jnp.concatenate(wide, axis=0), preferred_element_type=F32)
             return 0
 
-        lax.fori_loop(0, 8, body, 0)
+        lax.fori_loop(begin, end, body, 0)
 
     near = (lax.broadcasted_iota(jnp.int32, (384, 128), 1) & 16) == 0
 
@@ -262,78 +303,104 @@
             )
 
     z_copies = []
-    group_sums(0)
+    group_sums(0, 0, 4)
+    lc.wait_recv()
+    lsend[2] = lsend[1] + lrc[...]
+    lz = [start(remote(lsend.at[2, half], lrz.at[k], l_send.at[1, k], l_recv.at[1, k], z_peers[k])) for k in range(1, 8)]
+    group_sums(0, 4, 8)
     send_sums(0)
+    for copy in g2:
+        copy.wait_recv()
+    g3 = [
+        start(remote(gbuf.at[:, :, ci, quarter], gbuf.at[:, :, ci, quarter], g_send.at[2, o], g_recv.at[2, o], x_peers[o]))
+        for o in range(3)
+    ]
 
     group_sums(1)
     send_sums(1)
     for copy in lz:
         copy.wait_recv()
-    lsend[2] = lsend[1] + sum(lrz[k] for k in range(1, 8))
-    ly = [start(remote(lsend.at[2], lry.at[k], l_send.at[2, k], l_recv.at[2, k], y_peers[k])) for k in range(1, 8)]
+    half_lib[...] = lsend[2, half, :] + sum(lrz[k] for k in range(1, 8))
+    ly = [
+        start(remote(half_lib, lry.at[o], l_send.at[2, o], l_recv.at[2, o], {Y: moved(Y, off)}))
+        for o, off in enumerate(OFFS)
+    ]
     send_pieces(3)
-    for copy in g2:
-        copy.wait_recv()
-    g3 = [
-        start(remote(gbuf.at[:, :, ci, quarter], gbuf.at[:, :, ci, quarter], g_send.at[2, o], g_recv.at[2, o], x_peers[o]))
-        for o in range(3)
-    ]
 
     group_sums(2)
     send_sums(2)
-
-    group_sums(3)
     for copy in g3:
         copy.wait_recv()
     g4 = start(remote(gbuf.at[:, :, ci], gbuf.at[:, :, ci], g_send.at[3, 0], g_recv.at[3, 0], {CORE: 1 - ci}))
+
+    group_sums(3, 0, 4)
     for copy in ly:
         copy.wait_recv()
-    library_parts = three_parts(jnp.maximum(lsend[2] + sum(lry[k] for k in range(1, 8)), 1.0))
+    library[half, :] = half_lib[...] + lry[0] + lry[1] + lry[2]
+    ll = start(remote(library.at[half], library.at[half], l_send.at[2, 3], l_recv.at[2, 3], {CORE: 1 - ci}))
+    group_sums(3, 4, 8)
+    ll.wait_recv()
+    library_parts = three_parts(jnp.maximum(library[...], 1.0))
     g4.wait_recv()
-    geno_out = pltpu.make_async_copy(gbuf, geno_ref, out_sem)
+    geno_out = pltpu.make_async_copy(gbuf, geno_ref, out_sem.at[3])
     geno_out.start()
     for copy in z_copies[2:]:
         copy.wait_recv()
     type_row = lax.broadcasted_iota(jnp.int32, (32, 256), 0)
     tl = lax.broadcasted_iota(jnp.int32, (32, 256), 1) // 32
     here = near[:128]
+    stores = [geno_out]
+
+    def std_store(t):
+        at_rows = pl.ds(t * 256, 256)
+        return pltpu.make_async_copy(std.at[at_rows], std_ref.at[at_rows], out_sem.at[t])
+
     for t in range(3):
         at_rows = pl.ds(t * 128, 128)
         expand = jnp.where(type_row == tl + 8 * t, 1.0, 0.0).astype(BF16)
-        library = sum(lax.dot_general(part, expand, TN, preferred_element_type=F32) for part in library_parts)
+        size = sum(lax.dot_general(part, expand, TN, preferred_element_type=F32) for part in library_parts)
         a = decoded(zrecv[1, 0, at_rows, :]) + decoded(zrecv[2, 1, at_rows, :])
         b = decoded(zrecv[2, 0, at_rows, :]) + decoded(zrecv[1, 1, at_rows, :])
         others = [jnp.where(here, a, pltpu.roll(b, 16, 1)), jnp.where(here, pltpu.roll(a, 112, 1), b)]
         pseudo = acc[at_rows, :] + jnp.concatenate(others, axis=1)
-        logged = jnp.log1p(10000.0 * pseudo / library)
+        logged = jnp.log1p(10000.0 * pseudo / size)
         spread = logged - jnp.mean(logged, axis=0, keepdims=True)
         standard = spread * lax.rsqrt(jnp.mean(spread * spread, axis=0, keepdims=True) + 1e-06)
-        std_ref[pl.ds(t * 256, 256), :] = jnp.transpose(standard).astype(BF16)
-    geno_out.wait()
+        std[pl.ds(t * 256, 256), :] = jnp.transpose(standard).astype(BF16)
+        stores.append(std_store(t))
+        stores[-1].start()
+    for copy in stores:
+        copy.wait()
     for copy in pending:
         copy.wait_send()
 
 
-def scores_kernel(std_ref, geno_ref, out_ref, buffer, sem):
-    def store(i):
-        columns = pl.ds(pl.multiple_of(i * COLUMNS, COLUMNS), COLUMNS)
-        return pltpu.make_async_copy(buffer.at[i], out_ref.at[:, columns], sem.at[i])
-
-    def body(i, _):
-        count = COLUMNS // 128
-        geno = jnp.concatenate([geno_ref[i * count + j] for j in range(count)], axis=1)
+def scores_kernel(std_hbm, geno_hbm, out_ref, std_ref, geno_ref, buffer, in_sem, sem):
+    loads = [pltpu.make_async_copy(std_hbm, std_ref, in_sem.at[len(BANDS)])]
+    stores = []
+    begin = 0
+    for i, width in enumerate(BANDS):
+        blocks = pl.ds(begin // 128, width // 128)
+        loads.append(pltpu.make_async_copy(geno_hbm.at[blocks], geno_ref.at[blocks], in_sem.at[i]))
+        columns = pl.ds(begin, width)
+        stores.append(pltpu.make_async_copy(buffer.at[:, columns], out_ref.at[:, columns], sem.at[i]))
+        begin += width
+    for copy in loads:
+        copy.start()
+    loads[0].wait()
+    begin = 0
+    for i, width in enumerate(BANDS):
+        loads[i + 1].wait()
+        geno = jnp.concatenate([geno_ref[begin // 128 + j] for j in range(width // 128)], axis=1)
         product = jnp.dot(std_ref[...], geno, preferred_element_type=F32) * DONORS ** (-0.5)
-        buffer[i] = product.astype(BF16)
-        store(i).start()
-        return 0
-
-    steps = buffer.shape[0]
-    lax.fori_loop(0, steps, body, 0)
-    lax.fori_loop(0, steps, lambda i, _: (store(i).wait(), 0)[1], 0)
+        buffer[:, pl.ds(begin, width)] = product.astype(BF16)
+        stores[i].start()
+        begin += width
+    for copy in stores:
+        copy.wait()
 
 
 def on_device(umi_counts, cell_donors, cell_types, live_cells, dosages):
-    vmem = pl.BlockSpec(memory_space=pltpu.VMEM)
     hbm = pl.BlockSpec(memory_space=pl.ANY)
     dma = pltpu.SemaphoreType.DMA
     standard, geno = pl.pallas_call(
@@ -343,9 +410,13 @@
             jax.ShapeDtypeStruct((768, 128), BF16),
             jax.ShapeDtypeStruct((4, 4, 2, 128, 128), BF16),
         ),
-        in_specs=[pl.BlockSpec(memory_space=pltpu.SMEM), hbm, vmem, vmem, vmem],
-        out_specs=(vmem, hbm),
+        in_specs=[pl.BlockSpec(memory_space=pltpu.SMEM)] + [hbm] * 4,
+        out_specs=(hbm, hbm),
         scratch_shapes=[
+            pltpu.VMEM((8, 128), jnp.int32),
+            pltpu.VMEM((8, 128), jnp.int32),
+            pltpu.VMEM((DONORS, 128), jnp.int32),
+            pltpu.VMEM((768, 128), BF16),
             pltpu.VMEM((4, 1024, 256), jnp.int32),
             pltpu.VMEM((4, 8, 256, 128), BF16),
             pltpu.VMEM((4, 8, 256, 128), BF16),
@@ -360,10 +431,13 @@
             pltpu.VMEM((4, 4, 2, 128, 128), BF16),
             pltpu.VMEM((3, 32, 128), F32),
             pltpu.VMEM((3, 32, 128), F32),
-            pltpu.VMEM((8, 32, 128), F32),
-            pltpu.VMEM((8, 32, 128), F32),
-            dma((4,)), dma((4, 8)), dma((4, 8)), dma((8,)), dma((8,)), dma((4, 3)), dma((4, 3)),
-            dma((3, 8)), dma((3, 8)), dma((3, 2)), dma((3, 2)), dma,
+            pltpu.VMEM((32, 128), F32),
+            pltpu.VMEM((8, 16, 128), F32),
+            pltpu.VMEM((3, 16, 128), F32),
+            pltpu.VMEM((16, 128), F32),
+            pltpu.VMEM((32, 128), F32),
+            dma((11,)), dma((5, 8)), dma((5, 8)), dma((8,)), dma((8,)), dma((4, 3)), dma((4, 3)),
+            dma((3, 8)), dma((3, 8)), dma((3, 2)), dma((3, 2)), dma((3,)), dma((4,)),
         ],
         compiler_params=pltpu.CompilerParams(
             collective_id=0, has_side_effects=True, vmem_limit_bytes=VMEM_LIMIT
@@ -374,9 +448,14 @@
         scores_kernel,
         name="scores",
         out_shape=jax.ShapeDtypeStruct((768, 4096), BF16),
-        in_specs=[vmem, vmem],
+        in_specs=[hbm, hbm],
         out_specs=hbm,
-        scratch_shapes=[pltpu.VMEM((4096 // COLUMNS, 768, COLUMNS), BF16), dma((4096 // COLUMNS,))],
+        scratch_shapes=[
+            pltpu.VMEM((768, 128), BF16),
+            pltpu.VMEM((32, 128, 128), BF16),
+            pltpu.VMEM((768, 4096), BF16),
+            dma((len(BANDS) + 1,)), dma((len(BANDS),)),
+        ],
         compiler_params=pltpu.CompilerParams(vmem_limit_bytes=VMEM_LIMIT),
     )(standard, geno)
     return scores.reshape(TYPES, 32, 4096)

time: 49.5 us -> 46.6 us (0.941)
  Pallas kernels: 48.6 us -> 45.8 us
    pallas_call x1, Pallas kernels: 43.8 us -> 41.2 us  [on_device(): pl.pallas_call(gather_kernel, name='gather', out_shape=(jax.ShapeDtypeStr...]
where the time goes in v3:
time: 46.6 us; the launch traced here: 46.4 us
  Pallas kernels  45.8 us (98%)
  between operations  0.66 us (1%)
    pallas_call x1, Pallas kernels, on_device(): pl.pallas_call(gather_kernel, name='gather', out_shape=(jax.ShapeDtypeStr...  41.2 us
    pallas_call x1, Pallas kernels, on_device(): pl.pallas_call(scores_kernel, name='scores', out_shape=jax.ShapeDtypeStru...  4.62 us

profile of v3, /device:TPU:1, one launch (start us, length us, event | category | flops | bytes accessed | tf_op | source)
XLA Modules:
  0.0 46.4 jit_solution(4123304223525536517)
XLA Ops:
  0.7 41.2 %gather.1 = (bf16[768,128]{1,0:T(8,128)(2,1)}, bf16[4,4,2,128,128]{4,3,2,1,0:T(8,128)(2,1)}) custom-call(s32[1]{0:T(128)S(6)} %copy.6.live_ref, s32[1024,1024]{1,0:T(8,128)} %umi_ref.1, s32[8,128]{1,0:T(8,128)} %bitcast.5, s32[8,128]{1,0:T(8,128)} %bitcast.6, s32[128,128]{1,0:T(8,128)} %dosages_hbm.1), custom_call_target="tpu_custom_call" | custom-call | tf_op jit(solution)/shard_map/gather/pallas_call | solution.py:406
  41.8 4.6 %scores.1 = bf16[768,4096]{1,0:T(8,128)(2,1)} custom-call(bf16[768,128]{1,0:T(8,128)(2,1)} %get-tuple-element.7.std_hbm, bf16[32,128,128]{2,1,0:T(8,128)(2,1)} %bitcast.4), custom_call_target="tpu_custom_call" | custom-call | tf_op jit(solution)/shard_map/scores/pallas_call | solution.py:447

commit v4 on v3

--- a/solution.py
+++ b/solution.py
@@ -50,7 +50,7 @@
     live_ref, umi_ref, donors_hbm, types_hbm, dosages_hbm,
     std_ref, geno_ref,
     donors_ref, types_ref, dosages_ref, std,
-    xin, sendb, recvb, codeb, onehot, mask, acc, zsend, zrecv, rows, gown, gbuf, lsend, lrx, lrc, lrz, lry, half_lib, library,
+    xin, sendb, recvb, codeb, onehot, mask, acc, zsend, zrecv, rows, gown, gbuf, lsend, lrx, lrc, lrz, lry, half_lib, library, scale,
     in_sem, d_send, d_recv, c_send, c_recv, g_send, g_recv, l_send, l_recv, z_send, z_recv, small_sem, out_sem,
 ):
     at = {axis: lax.axis_index(axis) for axis in AXES}
@@ -284,25 +284,34 @@
 
         lax.fori_loop(begin, end, body, 0)
 
-    near = (lax.broadcasted_iota(jnp.int32, (384, 128), 1) & 16) == 0
+    near = (lax.broadcasted_iota(jnp.int32, (DONORS, 128), 1) & 16) == 0
+    high_rows = [pl.ds(t * DONORS, DONORS) for t in range(3)]
 
     def send_sums(c):
-        lower, upper = acc[:, pl.ds(0, 128)], acc[:, pl.ds(128, 128)]
-        a = jnp.where(near, lower, pltpu.roll(upper, 16, 1))
-        b = jnp.where(near, pltpu.roll(lower, 112, 1), upper)
-        up, down_ = (a, b) if c == 1 else (b, a)
-        if c == 2:
-            for copy in z_copies[:2]:
-                copy.wait_recv()
-            up, down_ = up + decoded(zrecv[0, 0]), down_ + decoded(zrecv[0, 1])
-        zsend[c, 0] = coded(up)
-        zsend[c, 1] = coded(down_)
-        for d, off in enumerate((1, 3)):
-            z_copies.append(
-                start(remote(zsend.at[c, d], zrecv.at[c, d], z_send.at[c, d], z_recv.at[c, d], {Z: moved(Z, off)}))
-            )
-
-    z_copies = []
+        for t, at_rows in enumerate(high_rows):
+            lower, upper = acc[at_rows, pl.ds(0, 128)], acc[at_rows, pl.ds(128, 128)]
+            a = jnp.where(near, lower, pltpu.roll(upper, 16, 1))
+            b = jnp.where(near, pltpu.roll(lower, 112, 1), upper)
+            sums = (a, b) if c == 1 else (b, a)
+            for d, off in enumerate((1, 3)):
+                value = sums[d]
+                if c == 2:
+                    z_copies[0, d, t].wait_recv()
+                    value = value + decoded(zrecv[0, d, at_rows, :])
+                zsend[c, d, at_rows, :] = coded(value)
+                z_copies[c, d, t] = start(
+                    remote(
+                        zsend.at[c, d, at_rows], zrecv.at[c, d, at_rows],
+                        z_send.at[c, 3 * d + t], z_recv.at[c, 3 * d + t], {Z: moved(Z, off)},
+                    )
+                )
+
+    def merged(a, b):
+        return jnp.concatenate(
+            [jnp.where(near, a, pltpu.roll(b, 16, 1)), jnp.where(near, pltpu.roll(a, 112, 1), b)], axis=1
+        )
+
+    z_copies = {}
     group_sums(0, 0, 4)
     lc.wait_recv()
     lsend[2] = lsend[1] + lrc[...]
@@ -333,41 +342,40 @@
         copy.wait_recv()
     g4 = start(remote(gbuf.at[:, :, ci], gbuf.at[:, :, ci], g_send.at[3, 0], g_recv.at[3, 0], {CORE: 1 - ci}))
 
-    group_sums(3, 0, 4)
     for copy in ly:
         copy.wait_recv()
     library[half, :] = half_lib[...] + lry[0] + lry[1] + lry[2]
     ll = start(remote(library.at[half], library.at[half], l_send.at[2, 3], l_recv.at[2, 3], {CORE: 1 - ci}))
-    group_sums(3, 4, 8)
-    ll.wait_recv()
-    library_parts = three_parts(jnp.maximum(library[...], 1.0))
+
+    group_sums(3, 0, 4)
     g4.wait_recv()
     geno_out = pltpu.make_async_copy(gbuf, geno_ref, out_sem.at[3])
     geno_out.start()
-    for copy in z_copies[2:]:
-        copy.wait_recv()
+    ll.wait_recv()
+    library_parts = three_parts(jnp.maximum(library[...], 1.0))
     type_row = lax.broadcasted_iota(jnp.int32, (32, 256), 0)
     tl = lax.broadcasted_iota(jnp.int32, (32, 256), 1) // 32
-    here = near[:128]
-    stores = [geno_out]
-
-    def std_store(t):
-        at_rows = pl.ds(t * 256, 256)
-        return pltpu.make_async_copy(std.at[at_rows], std_ref.at[at_rows], out_sem.at[t])
-
-    for t in range(3):
-        at_rows = pl.ds(t * 128, 128)
+    for t, at_rows in enumerate(high_rows):
         expand = jnp.where(type_row == tl + 8 * t, 1.0, 0.0).astype(BF16)
         size = sum(lax.dot_general(part, expand, TN, preferred_element_type=F32) for part in library_parts)
-        a = decoded(zrecv[1, 0, at_rows, :]) + decoded(zrecv[2, 1, at_rows, :])
-        b = decoded(zrecv[2, 0, at_rows, :]) + decoded(zrecv[1, 1, at_rows, :])
-        others = [jnp.where(here, a, pltpu.roll(b, 16, 1)), jnp.where(here, pltpu.roll(a, 112, 1), b)]
-        pseudo = acc[at_rows, :] + jnp.concatenate(others, axis=1)
-        logged = jnp.log1p(10000.0 * pseudo / size)
+        scale[at_rows, :] = 10000.0 / size
+    for t, at_rows in enumerate(high_rows):
+        for d in range(2):
+            z_copies[1, d, t].wait_recv()
+        acc[at_rows, :] += merged(decoded(zrecv[1, 0, at_rows, :]), decoded(zrecv[1, 1, at_rows, :]))
+    group_sums(3, 4, 8)
+    stores = [geno_out]
+    for t in range(3):
+        for d in range(2):
+            z_copies[2, d, t].wait_recv()
+    for t, at_rows in enumerate(high_rows):
+        pseudo = acc[at_rows, :] + merged(decoded(zrecv[2, 1, at_rows, :]), decoded(zrecv[2, 0, at_rows, :]))
+        logged = jnp.log1p(pseudo * scale[at_rows, :])
         spread = logged - jnp.mean(logged, axis=0, keepdims=True)
         standard = spread * lax.rsqrt(jnp.mean(spread * spread, axis=0, keepdims=True) + 1e-06)
-        std[pl.ds(t * 256, 256), :] = jnp.transpose(standard).astype(BF16)
-        stores.append(std_store(t))
+        to_rows = pl.ds(t * 256, 256)
+        std[to_rows, :] = jnp.transpose(standard).astype(BF16)
+        stores.append(pltpu.make_async_copy(std.at[to_rows], std_ref.at[to_rows], out_sem.at[t]))
         stores[-1].start()
     for copy in stores:
         copy.wait()
@@ -436,8 +444,9 @@
             pltpu.VMEM((3, 16, 128), F32),
             pltpu.VMEM((16, 128), F32),
             pltpu.VMEM((32, 128), F32),
+            pltpu.VMEM((384, 256), F32),
             dma((11,)), dma((5, 8)), dma((5, 8)), dma((8,)), dma((8,)), dma((4, 3)), dma((4, 3)),
-            dma((3, 8)), dma((3, 8)), dma((3, 2)), dma((3, 2)), dma((3,)), dma((4,)),
+            dma((3, 8)), dma((3, 8)), dma((3, 6)), dma((3, 6)), dma((3,)), dma((4,)),
         ],
         compiler_params=pltpu.CompilerParams(
             collective_id=0, has_side_effects=True, vmem_limit_bytes=VMEM_LIMIT

time: 46.6 us -> 46.4 us (level)
  no operation moved by 1% of the time
where the time goes in v4:
time: 46.4 us; the launch traced here: 46.3 us
  Pallas kernels  45.6 us (98%)
  between operations  0.66 us (1%)
    pallas_call x1, Pallas kernels, on_device(): pl.pallas_call(gather_kernel, name='gather', out_shape=(jax.ShapeDtypeStr...  41 us
    pallas_call x1, Pallas kernels, on_device(): pl.pallas_call(scores_kernel, name='scores', out_shape=jax.ShapeDtypeStru...  4.62 us

profile of v4, /device:TPU:1, one launch (start us, length us, event | category | flops | bytes accessed | tf_op | source)
XLA Modules:
  0.0 46.3 jit_solution(1335629874770499903)
XLA Ops:
  0.7 41.0 %gather.1 = (bf16[768,128]{1,0:T(8,128)(2,1)}, bf16[4,4,2,128,128]{4,3,2,1,0:T(8,128)(2,1)}) custom-call(s32[1]{0:T(128)S(6)} %copy.6.live_ref, s32[1024,1024]{1,0:T(8,128)} %umi_ref.1, s32[8,128]{1,0:T(8,128)} %bitcast.5, s32[8,128]{1,0:T(8,128)} %bitcast.6, s32[128,128]{1,0:T(8,128)} %dosages_hbm.1), custom_call_target="tpu_custom_call" | custom-call | tf_op jit(solution)/shard_map/gather/pallas_call | solution.py:414
  41.7 4.6 %scores.1 = bf16[768,4096]{1,0:T(8,128)(2,1)} custom-call(bf16[768,128]{1,0:T(8,128)(2,1)} %get-tuple-element.7.std_hbm, bf16[32,128,128]{2,1,0:T(8,128)(2,1)} %bitcast.4), custom_call_target="tpu_custom_call" | custom-call | tf_op jit(solution)/shard_map/scores/pallas_call | solution.py:456

commit v5 on v4

--- a/solution.py
+++ b/solution.py
@@ -255,17 +255,21 @@
 
     quad = (lax.broadcasted_iota(jnp.int32, (256, 128), 1) // 32).astype(F32).astype(BF16)
 
+    wrapped = (3 - yi) // 3
+
     def group_sums(c, begin=0, end=8):
         if begin == 0:
             acc[...] = jnp.zeros_like(acc)
 
-        def body(s, _):
-            @pl.when(s > 0)
+        def body(i, _):
+            s = i + wrapped * (i // 4) * (2 - 4 * (i % 4 // 2))
+
+            @pl.when(i > 0)
             def _():
                 if c == 0:
-                    for i in range(2):
-                        part = recvb.at[0, s, pl.ds(i * 128, 128)]
-                        remote(part, part, d_send.at[4 * i, s], d_recv.at[4 * i, s], y_peers[1]).wait_recv()
+                    for j in range(2):
+                        part = recvb.at[0, s, pl.ds(j * 128, 128)]
+                        remote(part, part, d_send.at[4 * j, s], d_recv.at[4 * j, s], y_peers[1]).wait_recv()
                 else:
                     remote(recvb.at[c, s], recvb.at[c, s], d_send.at[c, s], d_recv.at[c, s], y_peers[1]).wait_recv()
 

time: 46.4 us -> 46.2 us (level)
  no operation moved by 1% of the time
where the time goes in v5:
time: 46.2 us; the launch traced here: 46.1 us
  Pallas kernels  45.4 us (98%)
  between operations  0.66 us (1%)
    pallas_call x1, Pallas kernels, on_device(): pl.pallas_call(gather_kernel, name='gather', out_shape=(jax.ShapeDtypeStr...  40.8 us
    pallas_call x1, Pallas kernels, on_device(): pl.pallas_call(scores_kernel, name='scores', out_shape=jax.ShapeDtypeStru...  4.63 us

profile of v5, /device:TPU:1, one launch (start us, length us, event | category | flops | bytes accessed | tf_op | source)
XLA Modules:
  0.0 46.1 jit_solution(322446684083838255)
XLA Ops:
  0.7 40.8 %gather.1 = (bf16[768,128]{1,0:T(8,128)(2,1)}, bf16[4,4,2,128,128]{4,3,2,1,0:T(8,128)(2,1)}) custom-call(s32[1]{0:T(128)S(6)} %copy.6.live_ref, s32[1024,1024]{1,0:T(8,128)} %umi_ref.1, s32[8,128]{1,0:T(8,128)} %bitcast.5, s32[8,128]{1,0:T(8,128)} %bitcast.6, s32[128,128]{1,0:T(8,128)} %dosages_hbm.1), custom_call_target="tpu_custom_call" | custom-call | tf_op jit(solution)/shard_map/gather/pallas_call | solution.py:418
  41.4 4.6 %scores.1 = bf16[768,4096]{1,0:T(8,128)(2,1)} custom-call(bf16[768,128]{1,0:T(8,128)(2,1)} %get-tuple-element.7.std_hbm, bf16[32,128,128]{2,1,0:T(8,128)(2,1)} %bitcast.4), custom_call_target="tpu_custom_call" | custom-call | tf_op jit(solution)/shard_map/scores/pallas_call | solution.py:460
